TPU v7x, 32 devices: a whole 2x2x4 slice. The times are simulated.
32 devices in a mesh: dp: 8 (over y, x, core), mp: 4 (over z).
Axes of the slice: x: 2, y: 2, z: 4, core: 2. Of those that a mesh axis runs over, the one named last changes fastest.
Arguments:
- hidden: bfloat16 [16384, 13824], P('dp', 'mp'), may hold values from -6 to 6
- out_grad: bfloat16 [16384, 5120], P('dp', 'mp'), may hold values from -6 to 6
- proj_in: bfloat16 [64, 13824], P(None, 'mp'), may hold values from -0.0546875 to 0.0546875
- proj_out: bfloat16 [64, 5120], P(None, 'mp'), may hold values from -0.078125 to 0.078125
- segment_ids: int32 [8, 2048], P('dp'), may hold values from 0 to 15, never falling along the last dimension, each value on 1 to 1024 neighbouring positions
Outputs:
- features: float32 [128, 4096], P('dp')
- gram: float32 [4096, 4096], P(('dp', 'mp'))
Inputs may be any that keep to these rules, and one draw needn't show every extreme that they name: `segment_ids`: within each row the numbers never fall; each of the 16 numbers names 1 to 1024 tokens of the row.
All inputs are finite; a program needn't handle non-finite values.
Results may differ from a plain program's by a relative error of at most 0.0003.
Values sent between devices are 32-bit elements; how exact they have to be, the bound alone decides.
No kernel may reach another device: no remote copies, remote signals or barrier semaphores. Data moves between devices by JAX's collectives and lax.ppermute only.
A program may use at most 64 MiB of HBM per device.

v0:
```python
import jax
import jax.numpy as jnp
from jax import lax
from jax.sharding import PartitionSpec as P

EX_DEV = 16


def outer_sums(onehot, projected, width):
    inputs = projected[:, :width]
    outputs = projected[:, width:]
    weighted = onehot[:, :, None] * outputs[None, :, :]
    grads = jnp.einsum("eti,tj->eij", weighted, inputs, precision=lax.Precision.HIGHEST)
    return grads.reshape(onehot.shape[0], width * width)


def body(hidden, out_grad, proj_in, proj_out, segment_ids):
    width = proj_in.shape[0]
    examples = EX_DEV
    inputs = lax.dot_general(
        hidden, proj_in, (((1,), (1,)), ((), ())), preferred_element_type=jnp.float32
    )
    outputs = lax.dot_general(
        out_grad, proj_out, (((1,), (1,)), ((), ())), preferred_element_type=jnp.float32
    )
    projected = jnp.concatenate([inputs, outputs], axis=1)
    example_ids = segment_ids[0]
    onehot = (example_ids[None, :] == jnp.arange(examples, dtype=jnp.int32)[:, None]).astype(
        jnp.float32
    )
    counts = jnp.sum(onehot, axis=1)
    summed = lax.psum(projected, "mp")
    grads = outer_sums(onehot, summed, width)
    features = grads / jnp.sqrt(counts)[:, None]
    proj_size = width * width
    data_count = lax.axis_size("dp")
    model_count = lax.axis_size("mp")
    row_count = proj_size // (data_count * model_count)
    total_examples = examples * data_count
    col_first = (lax.axis_index("dp") * model_count + lax.axis_index("mp")) * row_count
    shard_piece = lax.all_gather(features, "dp", axis=0, tiled=True)
    left = lax.dynamic_slice_in_dim(shard_piece, col_first, row_count, 1)
    gram_rows = lax.dot_general(
        left,
        shard_piece,
        (((0,), (0,)), ((), ())),
        precision=lax.Precision.HIGHEST,
        preferred_element_type=jnp.float32,
    )
    return (features, gram_rows / total_examples)


def solution(mesh):
    placed = (P("dp", "mp"), P("dp", "mp"), P(None, "mp"), P(None, "mp"), P("dp", None))
    return jax.shard_map(
        body,
        mesh=mesh,
        in_specs=placed,
        out_specs=(P("dp", None), P(("dp", "mp"), None)),
        check_vma=False,
    )
```

profile of v0, /device:TPU:0, one launch (start us, length us, event | category | flops | bytes accessed | tf_op | source)
XLA Modules:
  0.0 124.1 jit_solution(2751535235130744079)
XLA Ops:
  7.2 0.0 copy-start
  7.2 0.0 copy-start.2
  7.2 0.0 all-reduce.2.cloned.1.call-start
  7.2 0.9 copy-done
  8.2 0.0 copy-start.1
  8.2 9.5 %fusion.8 = f32[2048,64]{0,1:T(8,128)S(1)} fusion(bf16[2048,3456]{1,0:T(8,128)(2,1)} %param.5, bf16[64,3456]{1,0:T(8,128)(2,1)S(1)} %copy-done), kind=kOutput, calls=%fused_computation.13 | convolution fusion | flops 905969664 | bytes 15122432 | tf_op jit(solution)/shard_map/dot_general | solution.py:20
  17.7 0.0 copy-done.2
  17.7 0.0 copy-done.1
  17.7 0.0 copy-start.3
  17.8 1.7 %fusion.9 = f32[2048,64]{0,1:T(8,128)S(1)} fusion(bf16[2048,1280]{1,0:T(8,128)(2,1)S(1)} %copy-done.1, bf16[64,1280]{1,0:T(8,128)(2,1)S(1)} %copy-done.2), kind=kOutput, calls=%fused_computation.14 | convolution fusion | flops 335544320 | bytes 5931008 | tf_op jit(solution)/shard_map/dot_general | solution.py:23
  19.4 1.1 pad_maximum_fusion
  20.5 0.0 all-reduce.2.cloned.1.call-update
  20.5 0.2 all-gather.2.cloned.1.call-start
  20.8 0.0 copy-done.3
  20.8 0.1 fusion.6
  20.9 54.4 %all-reduce.2.cloned.1.call-done = f32[2048,128]{0,1:T(8,128)} async-done(((f32[2048,128]{0,1:T(8,128)}), f32[2048,128]{0,1:T(8,128)}) %all-reduce.2.cloned.1.call-update) | async-done | bytes 1048592 | tf_op jit(solution)/shard_map/psum | solution.py:32
  75.4 1.1 slice.8
  76.4 7.7 %fusion = f32[16,64,64]{2,1,0:T(8,128)S(1)} fusion(f32[2048,64]{0,1:T(8,128)S(1)} %slice.8, f32[16,2048]{1,0:T(8,128)S(1)} %fusion.4, f32[2048,128]{0,1:T(8,128)} %all-reduce.2.cloned.1.call-done), kind=kOutput, calls=%fused_computation | convolution fusion | flops 1612709888 | bytes 1441792 | tf_op jit(solution)/shard_map/eti,tj->eij/dot_general | solution.py:13
  84.1 0.2 reshape.32
  84.3 0.8 broadcast_divide_fusion
  85.1 0.0 all-gather.2.cloned.1.call-update
  85.1 27.2 %all-gather.2.cloned.1.call-done = f32[128,4096]{1,0:T(8,128)} async-done(((f32[16,4096]{1,0:T(8,128)}), f32[128,4096]{1,0:T(8,128)}) %all-gather.2.cloned.1.call-update) | async-done | bytes 2097168 | tf_op jit(solution)/shard_map/all_gather | solution.py:41
  112.3 4.9 %convolution_multiply_fusion = f32[128,4096]{1,0:T(8,128)} fusion(f32[128,4096]{1,0:T(8,128)} %all-gather.2.cloned.1.call-done, s32[]{:T(128)S(6)} %select_n.3), kind=kOutput, calls=%fused_computation.2 | convolution fusion | flops 805830656 | bytes 4259844 | tf_op jit(solution)/shard_map/dot_general | solution.py:43
  (2 shorter events, 0.0 us)
Async XLA Ops:
  7.2 1.0 copy-start
  7.2 10.5 %copy-start.2 = (bf16[64,1280]{1,0:T(8,128)(2,1)S(1)}, bf16[64,1280]{1,0:T(8,128)(2,1)}, u32[]{:S(2)}) copy-start(bf16[64,1280]{1,0:T(8,128)(2,1)} %param.8) | copy-start | bytes 491524
  7.2 68.2 %all-reduce.2.cloned.1.call-start = ((), (), s32[]{:S(2)}) async-start(), calls=%async_computation | async-start | bytes 2097152 | tf_op jit(solution)/shard_map/psum | solution.py:32
  8.2 9.5 %copy-start.1 = (bf16[2048,1280]{1,0:T(8,128)(2,1)S(1)}, bf16[2048,1280]{1,0:T(8,128)(2,1)}, u32[]{:S(2)}) copy-start(bf16[2048,1280]{1,0:T(8,128)(2,1)} %param.6) | copy-start | bytes 15728644
  17.7 3.0 %copy-start.3 = (s32[1,2048]{1,0:T(1,128)S(1)}, s32[1,2048]{1,0:T(1,128)}, u32[]{:S(2)}) copy-start(s32[1,2048]{1,0:T(1,128)} %param.9) | copy-start | bytes 24580
  20.5 91.8 %all-gather.2.cloned.1.call-start = ((), (), s32[]{:S(2)}) async-start(), calls=%async_computation.1 | async-start | bytes 2359296 | tf_op jit(solution)/shard_map/all_gather | solution.py:41
Sparse Core Ops, SparseCore 0:
  20.6 54.6 all-reduce.1
  85.2 27.0 all-gather.1
where the time goes:
time: 124 us
  waiting for transfers between devices  81.7 us (66%)
  matrix products  23.8 us (19%)
  between operations  14.1 us (11%)
  local copies, waits for them, and re-layouts  2.24 us (2%)
  other arithmetic  2 us (2%)
    psum x1, waiting for transfers between devices, body(): summed = lax.psum(projected, 'mp')  54.4 us
    all_gather x1, waiting for transfers between devices, body(): shard_piece = lax.all_gather(features, 'dp', axis=0, tiled=True)  27.2 us
    dot_general x1, matrix products, body(): lax.dot_general(hidden, proj_in, (((1,), (1,)), ((), ())), preferred_elem...  9.53 us
    dot_general x1, matrix products, outer_sums(): jnp.einsum('eti,tj->eij', weighted, inputs, precision=lax.Precision.HIGHEST)  7.67 us
    dot_general x1, matrix products, body(): lax.dot_general(left, shard_piece, (((0,), (0,)), ((), ())), precision=la...  4.89 us
  transfers between devices with their start and end apart: 2, of which 2 were waited for; matrix products, arithmetic and copies ran while one was open for 0% of the time, Pallas kernels for 0%

commit v1 on v0

v1 whole, which is shorter than its diff:
```python
import functools

import jax
import jax.numpy as jnp
from jax import lax
from jax.experimental import pallas as pl
from jax.experimental.pallas import tpu as pltpu
from jax.sharding import PartitionSpec as P


EX_DEV = 16
NT = (((1,), (1,)), ((), ()))
HBM = pl.BlockSpec(memory_space=pltpu.HBM)
VMEM = pl.BlockSpec(memory_space=pltpu.VMEM)
SMEM = pl.BlockSpec(memory_space=pltpu.SMEM)


def in_hbm(x):
    return pltpu.with_memory_space_constraint(x, pltpu.HBM)


def in_vmem(x):
    return pltpu.with_memory_space_constraint(x, pltpu.VMEM)


def project_kernel(rows, x_ref, w_ref, out_ref, x_buf, w_buf, x_sem, w_sem):
    n = x_buf.shape[0]
    weights = pltpu.make_async_copy(w_ref, w_buf, w_sem)
    weights.start()
    halves = 2 if rows % 2 == 0 else 1
    size = rows // halves
    copies = [
        [
            pltpu.make_async_copy(
                x_ref.at[pl.ds(i * rows + h * size, size)],
                x_buf.at[i, pl.ds(h * size, size)],
                x_sem.at[i, h],
            )
            for h in range(halves)
        ]
        for i in range(n)
    ]

    def start(i):
        if i < n:
            for copy in copies[i]:
                copy.start()

    start(0)
    weights.wait()
    copies[0][0].wait()
    start(1)
    for copy in copies[0][1:]:
        copy.wait()
    for i in range(n):
        if i > 0:
            for copy in copies[i]:
                copy.wait()
        start(i + 2 if i > 0 else 2)
        out_ref[:, i * rows : (i + 1) * rows] = lax.dot_general(
            w_buf[...], x_buf[i], NT, preferred_element_type=jnp.float32
        )


def project(x, w, rows):
    tokens, depth = x.shape
    width = w.shape[0]
    rows = rows if tokens % rows == 0 else tokens
    n = tokens // rows
    return pl.pallas_call(
        functools.partial(project_kernel, rows),
        in_specs=[HBM, HBM],
        out_specs=VMEM,
        out_shape=pltpu.VMEM((width, tokens), jnp.float32),
        scratch_shapes=[
            pltpu.VMEM((n, rows, depth), x.dtype),
            pltpu.VMEM((width, depth), w.dtype),
            pltpu.SemaphoreType.DMA((n, 2)),
            pltpu.SemaphoreType.DMA,
        ],
        cost_estimate=pl.CostEstimate(
            flops=2 * tokens * depth * width,
            bytes_accessed=2 * tokens * depth,
            transcendentals=0,
        ),
        compiler_params=pltpu.CompilerParams(vmem_limit_bytes=24 << 20),
        name="project",
    )(in_hbm(x), in_hbm(w))


def split(x):
    high = x.astype(jnp.bfloat16)
    return high, (x - high.astype(jnp.float32)).astype(jnp.bfloat16)


def total(refs):
    return sum((r[...] for r in refs[1:]), refs[0][...])


def expand_kernel(n, examples, seg_ref, *refs):
    out_ref, scale_ref = refs[n:]
    tokens = seg_ref.shape[1]
    outputs = total(refs[:n])
    mask = (
        seg_ref[...] == lax.broadcasted_iota(jnp.int32, (examples, tokens), 0)
    ).astype(jnp.float32)
    high = outputs.astype(jnp.bfloat16).astype(jnp.float32)
    low = outputs - high
    width = outputs.shape[0]
    half = width * examples
    for i in range(width):
        first = i * examples
        rows = slice(first, first + examples)
        out_ref[rows, :] = (high[i : i + 1, :] * mask).astype(jnp.bfloat16)
        rows = slice(half + first, half + first + examples)
        out_ref[rows, :] = (low[i : i + 1, :] * mask).astype(jnp.bfloat16)
    scale_ref[...] = jnp.broadcast_to(
        1.0 / jnp.sqrt(jnp.sum(mask, axis=1, keepdims=True)), scale_ref.shape
    )


def expand(segment_ids, parts, examples):
    width, tokens = parts[0].shape
    n = len(parts)
    return pl.pallas_call(
        functools.partial(expand_kernel, n, examples),
        in_specs=[VMEM] * (1 + n),
        out_specs=[VMEM] * 2,
        out_shape=[
            pltpu.VMEM((2 * width * examples, tokens), jnp.bfloat16),
            pltpu.VMEM((examples, 128), jnp.float32),
        ],
        cost_estimate=pl.CostEstimate(
            flops=4 * width * examples * tokens,
            bytes_accessed=4 * width * examples * tokens,
            transcendentals=0,
        ),
        compiler_params=pltpu.CompilerParams(vmem_limit_bytes=24 << 20),
        name="expand",
    )(segment_ids, *parts)


def outer_kernel(n, examples, left_ref, scale_ref, *refs):
    input_refs, out_refs = refs[:n], refs[n:]
    width = input_refs[0].shape[0]
    right = jnp.concatenate(split(total(input_refs)), axis=0)
    scale = scale_ref[:, :width]
    half = width * examples
    rank = width // len(out_refs)
    rows = rank * examples
    for k, out_ref in enumerate(out_refs):

        def dot(first):
            return lax.dot_general(
                left_ref[first : first + rows, :], right, NT, preferred_element_type=jnp.float32
            )

        high, low = dot(k * rows), dot(half + k * rows)
        sums = high[:, :width] + high[:, width:] + low[:, :width]
        for i in range(rank):
            out_ref[:, i * width : (i + 1) * width] = (
                sums[i * examples : (i + 1) * examples] * scale
            )


def outer_sums(left, scale, inputs, cuts):
    examples = scale.shape[0]
    rows, tokens = left.shape
    width = inputs[0].shape[0]
    n = len(inputs)
    return pl.pallas_call(
        functools.partial(outer_kernel, n, examples),
        in_specs=[VMEM] * (2 + n),
        out_specs=[VMEM] * cuts,
        out_shape=[pltpu.VMEM((examples, width * width // cuts), jnp.float32)] * cuts,
        cost_estimate=pl.CostEstimate(
            flops=4 * rows * tokens * width,
            bytes_accessed=2 * rows * tokens,
            transcendentals=0,
        ),
        compiler_params=pltpu.CompilerParams(vmem_limit_bytes=24 << 20),
        name="outer_sums",
    )(in_vmem(left), in_vmem(scale), *inputs)


def gram_kernel(n, cuts, row_count, examples, block, first_ref, *refs):
    parts = refs[: n * cuts]
    features_ref, out_ref, terms, rows_ref, out_sem = refs[n * cuts :]
    size = parts[0].shape[1]
    total_examples = n * examples
    for k in range(n):
        high = slice(k * examples, (k + 1) * examples)
        low = slice(total_examples + k * examples, total_examples + (k + 1) * examples)
        for c in range(cuts):
            columns = slice(c * size, (c + 1) * size)
            part = parts[k * cuts + c][...]
            if k == 0:
                features_ref[:, columns] = part
            terms[high, columns], terms[low, columns] = split(part)
    lanes = rows_ref.shape[0]
    first = first_ref[0]
    base = pl.multiple_of(first // lanes * lanes, lanes)
    left_high = terms[:total_examples, pl.ds(base, lanes)].T
    left_low = terms[total_examples:, pl.ds(base, lanes)].T
    left_twice = jnp.concatenate([left_high, left_high], axis=1)
    offset = pl.multiple_of(first - base, row_count)

    def dot(a, b):
        return lax.dot_general(
            a, b, (((1,), (0,)), ((), ())), preferred_element_type=jnp.float32
        )

    copies = []
    for k in range(out_ref.shape[1] // block):
        columns = slice(k * block, (k + 1) * block)
        product = dot(left_twice, terms[:, columns]) + dot(
            left_low, terms[:total_examples, columns]
        )
        rows_ref[:, columns] = product * (1.0 / total_examples)
        copies.append(
            pltpu.make_async_copy(
                rows_ref.at[pl.ds(offset, row_count), columns], out_ref.at[:, columns], out_sem.at[k]
            )
        )
        copies[-1].start()
    for copy in copies:
        copy.wait()


def gram_rows(first, parts, row_count):
    n, cuts = len(parts), len(parts[0])
    examples = parts[0][0].shape[0]
    size = sum(x.shape[1] for x in parts[0])
    block = size // 4 if size % 512 == 0 else size
    return pl.pallas_call(
        functools.partial(gram_kernel, n, cuts, row_count, examples, block),
        in_specs=[SMEM] + [VMEM] * (n * cuts),
        out_specs=[VMEM, HBM],
        out_shape=[
            jax.ShapeDtypeStruct((examples, size), jnp.float32),
            jax.ShapeDtypeStruct((row_count, size), jnp.float32),
        ],
        scratch_shapes=[
            pltpu.VMEM((2 * n * examples, size), jnp.bfloat16),
            pltpu.VMEM((max(row_count, 128), size), jnp.float32),
            pltpu.SemaphoreType.DMA((size // block,)),
        ],
        cost_estimate=pl.CostEstimate(
            flops=6 * n * examples * row_count * size,
            bytes_accessed=4 * (n * examples + row_count) * size,
            transcendentals=0,
        ),
        compiler_params=pltpu.CompilerParams(vmem_limit_bytes=40 << 20),
        name="gram_rows",
    )(first, *[x for piece in parts for x in piece])


def body(hidden, out_grad, proj_in, proj_out, segment_ids):
    width = proj_in.shape[0]
    proj_size = width * width
    data = lax.axis_size("dp")
    model = lax.axis_size("mp")
    row_count = proj_size // (data * model)
    axes = ("dp", "mp")
    pair = 2 if data % 2 == 0 else 1
    groups = data // pair

    def owner(d):
        return min((model - 1) // 2 + d % pair, model - 1)

    def at(d, m):
        return d * model + (owner(d) + m) % model

    def hops(m):
        return max(abs((owner(d) + m) % model - owner(d)) for d in range(pair))

    others = sorted(range(1, model), key=hops)

    def to_owner(x):
        return [x] + [
            lax.ppermute(x, axes, [(at(d, m), at(d, 0)) for d in range(data)])
            for m in others
        ]

    def from_owner(x):
        return [
            lax.ppermute(x, axes, [(at(d, 0), at(d, m)) for d in range(data)])
            for m in others
        ]

    def other(g, k):
        return g ^ k if groups & (groups - 1) == 0 else (g + k) % groups

    def across(x, k):
        return lax.ppermute(
            x,
            "dp",
            [
                (g * pair + c, other(g, k) * pair + c)
                for g in range(groups)
                for c in range(pair)
            ],
        )

    def swap(x):
        return lax.ppermute(x, "dp", [(d, d ^ 1) for d in range(data)])

    d, m = lax.axis_index("dp"), lax.axis_index("mp")
    is_owner = m == jnp.minimum((model - 1) // 2 + d % pair, model - 1)

    outputs = project(out_grad, proj_out, 1024)
    outputs_sent = to_owner(outputs)
    inputs = project(hidden, proj_in, 512)
    inputs_sent = to_owner(inputs)
    left, scale = expand(segment_ids, outputs_sent, EX_DEV)
    pieces = []
    for summed in outer_sums(left, scale, inputs_sent, 2):
        features = jnp.where(is_owner, summed, sum(from_owner(summed)))
        parts = [features] + [across(features, k) for k in range(1, groups)]
        if pair == 2:
            parts = parts + [swap(x) for x in parts]
        pieces.append(parts)
    first = ((d * model + m) * row_count).astype(jnp.int32).reshape(1)
    features, gram = gram_rows(first, list(zip(*pieces)), row_count)
    return features, gram


def solution(mesh):
    placed = (P("dp", "mp"), P("dp", "mp"), P(None, "mp"), P(None, "mp"), P("dp", None))
    return jax.shard_map(
        body,
        mesh=mesh,
        in_specs=placed,
        out_specs=(P("dp", None), P(("dp", "mp"), None)),
        check_vma=False,
    )
```

time: 124 us -> 65.8 us (0.53)
  waiting for transfers between devices: 81.7 us -> 21.1 us
  starting transfers between devices: 0.26 us -> 25.4 us
  matrix products: 23.8 us -> 0 us
  Pallas kernels: 0 us -> 18 us
  between operations: 14.1 us -> 0.86 us
  local copies, waits for them, and re-layouts: 2.24 us -> 0.01 us
  other arithmetic: 2 us -> 0.06 us
    psum x1 -> x0, waiting for transfers between devices: 54.4 us -> none  [body(): summed = lax.psum(projected, 'mp')]
    all_gather x1 -> x0, waiting for transfers between devices: 27.2 us -> none  [body(): shard_piece = lax.all_gather(features, 'dp', axis=0, tiled=True)]
    ppermute x0 -> x26, starting transfers between devices: none -> 25.4 us  [the longest x6 10.8 us: to_owner(): lax.ppermute(x, axes, [(at(d, m), at(d, 0)) for d in range(data)])]
    dot_general x4 -> x0, matrix products: 23.8 us -> none  [the longest x1 9.53 us: body(): lax.dot_general(hidden, proj_in, (((1,), (1,)), ((), ())), preferred_elem...]
    ppermute x0 -> x26, waiting for transfers between devices: none -> 21.1 us  [the longest x6 8.93 us: to_owner(): lax.ppermute(x, axes, [(at(d, m), at(d, 0)) for d in range(data)])]
    pallas_call x0 -> x5, Pallas kernels: none -> 18 us  [the longest x2 11.4 us: project(): pl.pallas_call(functools.partial(project_kernel, rows), in_specs=[HBM, HB...]
  transfers between devices with their start and end apart: 2 -> 26, of which waited for: 2 -> 10; matrix products, arithmetic and copies ran while one was open for 0% -> 0% of each run, Pallas kernels for 0% -> 13%
where the time goes in v1:
time: 65.8 us; the launch traced here: 65.4 us
  starting transfers between devices  25.4 us (39%)
  waiting for transfers between devices  21.1 us (32%)
  Pallas kernels  18 us (27%)
  between operations  0.86 us (1%)
    pallas_call x2, Pallas kernels, project(): pl.pallas_call(functools.partial(project_kernel, rows), in_specs=[HBM, HB...  11.4 us
    ppermute x6, starting transfers between devices, to_owner(): lax.ppermute(x, axes, [(at(d, m), at(d, 0)) for d in range(data)])  10.8 us
    ppermute x6, waiting for transfers between devices, to_owner(): lax.ppermute(x, axes, [(at(d, m), at(d, 0)) for d in range(data)])  8.93 us
    ppermute x6, starting transfers between devices, across(): lax.ppermute(x, 'dp', [(g * pair + c, other(g, k) * pair + c) for g in ra...  8.1 us
    ppermute x6, waiting for transfers between devices, across(): lax.ppermute(x, 'dp', [(g * pair + c, other(g, k) * pair + c) for g in ra...  7.24 us
    ppermute x6, starting transfers between devices, from_owner(): lax.ppermute(x, axes, [(at(d, 0), at(d, m)) for d in range(data)])  5.24 us
    ppermute x6, waiting for transfers between devices, from_owner(): lax.ppermute(x, axes, [(at(d, 0), at(d, m)) for d in range(data)])  3.63 us
    pallas_call x1, Pallas kernels, gram_rows(): pl.pallas_call(functools.partial(gram_kernel, n, cuts, row_count, example...  2.7 us
  transfers between devices with their start and end apart: 26, of which 10 were waited for; matrix products, arithmetic and copies ran while one was open for 0% of the time, Pallas kernels for 13%

profile of v1, /device:TPU:0, one launch (start us, length us, event | category | flops | bytes accessed | tf_op | source)
XLA Modules:
  0.0 65.4 jit_solution(13594174284175944709)
XLA Ops:
  0.6 4.1 %project.2.refs_0_ = f32[64,2048]{1,0:T(8,128)S(1)} custom-call(bf16[2048,1280]{1,0:T(8,128)(2,1)} %x_ref.2, bf16[64,1280]{1,0:T(8,128)(2,1)} %w_ref.2), custom_call_target="tpu_custom_call" | custom-call | flops 335544320 | bytes 5242880 | tf_op jit(solution)/shard_map/project/pallas_call | solution.py:70
  4.7 0.7 %collective-permute-start = (f32[64,2048]{1,0:T(8,128)S(1)}, f32[64,2048]{1,0:T(8,128)S(1)}, u32[]{:S(2)}, u32[]{:S(2)}) collective-permute-start(f32[64,2048]{1,0:T(8,128)S(1)} %project.2.refs_0_), channel_id=1, source_target_pairs={{2,1},{7,6},{10,9},{15,14},{18,17},{23,22},{26,25},{31,30}} | collective-permute-start | bytes 1572872 | tf_op jit(solution)/shard_map/ppermute | solution.py:281
  5.4 5.6 %collective-permute-start.1 = (f32[64,2048]{1,0:T(8,128)S(1)}, f32[64,2048]{1,0:T(8,128)S(1)}, u32[]{:S(2)}, u32[]{:S(2)}) collective-permute-start(f32[64,2048]{1,0:T(8,128)S(1)} %project.2.refs_0_), channel_id=1, source_target_pairs={{0,1},{5,6},{8,9},{13,14},{16,17},{21,22},{24,25},{29,30}} | collective-permute-start | bytes 1572872 | tf_op jit(solution)/shard_map/ppermute | solution.py:281
  11.0 0.7 %collective-permute-start.2 = (f32[64,2048]{1,0:T(8,128)S(1)}, f32[64,2048]{1,0:T(8,128)S(1)}, u32[]{:S(2)}, u32[]{:S(2)}) collective-permute-start(f32[64,2048]{1,0:T(8,128)S(1)} %project.2.refs_0_), channel_id=1, source_target_pairs={{3,1},{4,6},{11,9},{12,14},{19,17},{20,22},{27,25},{28,30}} | collective-permute-start | bytes 1572872 | tf_op jit(solution)/shard_map/ppermute | solution.py:281
  11.7 7.3 %project.3.refs_0_ = f32[64,2048]{1,0:T(8,128)S(1)} custom-call(bf16[2048,3456]{1,0:T(8,128)(2,1)} %x_ref.3, bf16[64,3456]{1,0:T(8,128)(2,1)} %w_ref.3), custom_call_target="tpu_custom_call" | custom-call | flops 905969664 | bytes 14155776 | tf_op jit(solution)/shard_map/project/pallas_call | solution.py:70
  19.1 0.7 %collective-permute-start.3 = (f32[64,2048]{1,0:T(8,128)S(1)}, f32[64,2048]{1,0:T(8,128)S(1)}, u32[]{:S(2)}, u32[]{:S(2)}) collective-permute-start(f32[64,2048]{1,0:T(8,128)S(1)} %project.3.refs_0_), channel_id=1, source_target_pairs={{2,1},{7,6},{10,9},{15,14},{18,17},{23,22},{26,25},{31,30}} | collective-permute-start | bytes 1572872 | tf_op jit(solution)/shard_map/ppermute | solution.py:281
  19.8 2.5 %collective-permute-start.4 = (f32[64,2048]{1,0:T(8,128)S(1)}, f32[64,2048]{1,0:T(8,128)S(1)}, u32[]{:S(2)}, u32[]{:S(2)}) collective-permute-start(f32[64,2048]{1,0:T(8,128)S(1)} %project.3.refs_0_), channel_id=1, source_target_pairs={{0,1},{5,6},{8,9},{13,14},{16,17},{21,22},{24,25},{29,30}} | collective-permute-start | bytes 1572872 | tf_op jit(solution)/shard_map/ppermute | solution.py:281
  22.3 0.7 %collective-permute-start.5 = (f32[64,2048]{1,0:T(8,128)S(1)}, f32[64,2048]{1,0:T(8,128)S(1)}, u32[]{:S(2)}, u32[]{:S(2)}) collective-permute-start(f32[64,2048]{1,0:T(8,128)S(1)} %project.3.refs_0_), channel_id=1, source_target_pairs={{3,1},{4,6},{11,9},{12,14},{19,17},{20,22},{27,25},{28,30}} | collective-permute-start | bytes 1572872 | tf_op jit(solution)/shard_map/ppermute | solution.py:281
  23.0 1.4 %expand.1 = (bf16[2048,2048]{1,0:T(8,128)(2,1)S(1)}, f32[16,128]{1,0:T(8,128)S(1)}) custom-call(s32[1,2048]{1,0:T(1,128)S(1)} %copy-done, f32[64,2048]{1,0:T(8,128)S(1)} %project.2.refs_0_, f32[64,2048]{1,0:T(8,128)S(1)} %collective-permute-done.refs_1_, f32[64,2048]{1,0:T(8,128)S(1)} %collective-permute-done.1.refs_2_, ...), custom_call_target="tpu_custom_call" | custom-call | flops 8388608 | bytes 8388608 | tf_op jit(solution)/shard_map/expand/pallas_call | solution.py:125
  24.4 8.9 %collective-permute-done.4.refs_2_ = f32[64,2048]{1,0:T(8,128)S(1)} collective-permute-done((f32[64,2048]{1,0:T(8,128)S(1)}, f32[64,2048]{1,0:T(8,128)S(1)}, u32[]{:S(2)}, u32[]{:S(2)}) %collective-permute-start.4) | collective-permute-done | bytes 524320 | tf_op jit(solution)/shard_map/ppermute | solution.py:281
  33.3 2.5 %outer_sums.1 = (f32[16,2048]{1,0:T(8,128)S(1)}, f32[16,2048]{1,0:T(8,128)S(1)}) custom-call(bf16[2048,2048]{1,0:T(8,128)(2,1)S(1)} %get-tuple-element.6.left_ref, f32[16,128]{1,0:T(8,128)S(1)} %get-tuple-element.7.scale_ref, f32[64,2048]{1,0:T(8,128)S(1)} %project.3.refs_0_, f32[64,2048]{1,0:T(8,128)S(1)} %collective-permute-done.3.refs_1_, ...), custom_call_target="tpu_custom_call" | custom-call | flops 1073741824 | bytes 8388608 | tf_op jit(solution)/shard_map/outer_sums/pallas_call | solution.py:171
  35.8 1.3 %collective-permute-start.10 = (f32[16,2048]{1,0:T(8,128)S(1)}, f32[16,2048]{1,0:T(8,128)S(1)}, u32[]{:S(2)}, u32[]{:S(2)}) collective-permute-start(f32[16,2048]{1,0:T(8,128)S(1)} %get-tuple-element.9), channel_id=1, source_target_pairs={{1,0},{6,5},{9,8},{14,13},{17,16},{22,21},{25,24},{30,29}} | collective-permute-start | bytes 393224 | tf_op jit(solution)/shard_map/ppermute | solution.py:287
  39.2 1.3 %collective-permute-start.7 = (f32[16,2048]{1,0:T(8,128)S(1)}, f32[16,2048]{1,0:T(8,128)S(1)}, u32[]{:S(2)}, u32[]{:S(2)}) collective-permute-start(f32[16,2048]{1,0:T(8,128)S(1)} %get-tuple-element.8), channel_id=1, source_target_pairs={{1,0},{6,5},{9,8},{14,13},{17,16},{22,21},{25,24},{30,29}} | collective-permute-start | bytes 393224 | tf_op jit(solution)/shard_map/ppermute | solution.py:287
  40.5 2.7 %collective-permute-done.10 = f32[16,2048]{1,0:T(8,128)S(1)} collective-permute-done((f32[16,2048]{1,0:T(8,128)S(1)}, f32[16,2048]{1,0:T(8,128)S(1)}, u32[]{:S(2)}, u32[]{:S(2)}) %collective-permute-start.10) | collective-permute-done | bytes 131104 | tf_op jit(solution)/shard_map/ppermute | solution.py:287
  43.9 1.6 %collective-permute-start.13 = (f32[16,2048]{1,0:T(8,128)S(1)}, f32[16,2048]{1,0:T(8,128)S(1)}, u32[]{:S(2)}, u32[]{:S(2)}) collective-permute-start(f32[16,2048]{1,0:T(8,128)S(1)} %add_select_fusion.refs_1_), channel_id=1, source_target_pairs={{0,8},{4,12},{8,0},{12,4},{16,24},{20,28},{24,16},{28,20},{1,9},{5... | collective-permute-start | bytes 393224 | tf_op jit(solution)/shard_map/ppermute | solution.py:295
  45.4 1.5 %collective-permute-start.15 = (f32[16,2048]{1,0:T(8,128)S(1)}, f32[16,2048]{1,0:T(8,128)S(1)}, u32[]{:S(2)}, u32[]{:S(2)}) collective-permute-start(f32[16,2048]{1,0:T(8,128)S(1)} %add_select_fusion.refs_1_), channel_id=1, source_target_pairs={{0,16},{4,20},{8,24},{12,28},{16,0},{20,4},{24,8},{28,12},{1,17},{... | collective-permute-start | bytes 393224 | tf_op jit(solution)/shard_map/ppermute | solution.py:295
  47.4 1.0 %collective-permute-done.7 = f32[16,2048]{1,0:T(8,128)S(1)} collective-permute-done((f32[16,2048]{1,0:T(8,128)S(1)}, f32[16,2048]{1,0:T(8,128)S(1)}, u32[]{:S(2)}, u32[]{:S(2)}) %collective-permute-start.7) | collective-permute-done | bytes 131104 | tf_op jit(solution)/shard_map/ppermute | solution.py:287
  48.4 1.6 %collective-permute-start.12 = (f32[16,2048]{1,0:T(8,128)S(1)}, f32[16,2048]{1,0:T(8,128)S(1)}, u32[]{:S(2)}, u32[]{:S(2)}) collective-permute-start(f32[16,2048]{1,0:T(8,128)S(1)} %add_select_fusion.1.refs_0_), channel_id=1, source_target_pairs={{0,8},{4,12},{8,0},{12,4},{16,24},{20,28},{24,16},{28,20},{1,9},{5... | collective-permute-start | bytes 393224 | tf_op jit(solution)/shard_map/ppermute | solution.py:295
  50.1 1.5 %collective-permute-start.14 = (f32[16,2048]{1,0:T(8,128)S(1)}, f32[16,2048]{1,0:T(8,128)S(1)}, u32[]{:S(2)}, u32[]{:S(2)}) collective-permute-start(f32[16,2048]{1,0:T(8,128)S(1)} %add_select_fusion.1.refs_0_), channel_id=1, source_target_pairs={{0,16},{4,20},{8,24},{12,28},{16,0},{20,4},{24,8},{28,12},{1,17},{... | collective-permute-start | bytes 393224 | tf_op jit(solution)/shard_map/ppermute | solution.py:295
  51.7 3.0 %collective-permute-done.15.refs_5_ = f32[16,2048]{1,0:T(8,128)S(1)} collective-permute-done((f32[16,2048]{1,0:T(8,128)S(1)}, f32[16,2048]{1,0:T(8,128)S(1)}, u32[]{:S(2)}, u32[]{:S(2)}) %collective-permute-start.15) | collective-permute-done | bytes 131104 | tf_op jit(solution)/shard_map/ppermute | solution.py:295
  54.6 1.5 %collective-permute-start.16 = (f32[16,2048]{1,0:T(8,128)S(1)}, f32[16,2048]{1,0:T(8,128)S(1)}, u32[]{:S(2)}, u32[]{:S(2)}) collective-permute-start(f32[16,2048]{1,0:T(8,128)S(1)} %add_select_fusion.1.refs_0_), channel_id=1, source_target_pairs={{0,24},{4,28},{8,16},{12,20},{16,8},{20,12},{24,0},{28,4},{1,25},{... | collective-permute-start | bytes 393224 | tf_op jit(solution)/shard_map/ppermute | solution.py:295
  57.3 3.5 %collective-permute-done.16.refs_6_ = f32[16,2048]{1,0:T(8,128)S(1)} collective-permute-done((f32[16,2048]{1,0:T(8,128)S(1)}, f32[16,2048]{1,0:T(8,128)S(1)}, u32[]{:S(2)}, u32[]{:S(2)}) %collective-permute-start.16) | collective-permute-done | bytes 131104 | tf_op jit(solution)/shard_map/ppermute | solution.py:295
  61.4 0.8 %collective-permute-done.20.refs_10_ = f32[16,2048]{1,0:T(8,128)S(1)} collective-permute-done((f32[16,2048]{1,0:T(8,128)S(1)}, f32[16,2048]{1,0:T(8,128)S(1)}, u32[]{:S(2)}, u32[]{:S(2)}) %collective-permute-start.20) | collective-permute-done | bytes 131104 | tf_op jit(solution)/shard_map/ppermute | solution.py:306
  62.7 2.7 %gram_rows.1 = (f32[16,4096]{1,0:T(8,128)}, f32[128,4096]{1,0:T(8,128)}) custom-call(s32[1]{0:T(128)} %bitcast.first_ref, f32[16,2048]{1,0:T(8,128)S(1)} %add_select_fusion.1.refs_0_, f32[16,2048]{1,0:T(8,128)S(1)} %add_select_fusion.refs_1_, f32[16,2048]{1,0:T(8,128)S(1)} %collective-permute-done.12.refs_2_, ...), custom_call_target="tpu_custom_call" | custom-call | flops 402653184 | bytes 4194304 | tf_op jit(solution)/shard_map/gram_rows/pallas_call | solution.py:235
  (37 shorter events, 5.7 us)
Async XLA Ops:
  4.7 17.5 %collective-permute-start = (f32[64,2048]{1,0:T(8,128)S(1)}, f32[64,2048]{1,0:T(8,128)S(1)}, u32[]{:S(2)}, u32[]{:S(2)}) collective-permute-start(f32[64,2048]{1,0:T(8,128)S(1)} %project.2.refs_0_), channel_id=1, source_target_pairs={{2,1},{7,6},{10,9},{15,14},{18,17},{23,22},{26,25},{31,30}} | collective-permute-start | bytes 1572872 | tf_op jit(solution)/shard_map/ppermute | solution.py:281
  5.4 17.6 %collective-permute-start.1 = (f32[64,2048]{1,0:T(8,128)S(1)}, f32[64,2048]{1,0:T(8,128)S(1)}, u32[]{:S(2)}, u32[]{:S(2)}) collective-permute-start(f32[64,2048]{1,0:T(8,128)S(1)} %project.2.refs_0_), channel_id=1, source_target_pairs={{0,1},{5,6},{8,9},{13,14},{16,17},{21,22},{24,25},{29,30}} | collective-permute-start | bytes 1572872 | tf_op jit(solution)/shard_map/ppermute | solution.py:281
  11.0 12.0 %collective-permute-start.2 = (f32[64,2048]{1,0:T(8,128)S(1)}, f32[64,2048]{1,0:T(8,128)S(1)}, u32[]{:S(2)}, u32[]{:S(2)}) collective-permute-start(f32[64,2048]{1,0:T(8,128)S(1)} %project.2.refs_0_), channel_id=1, source_target_pairs={{3,1},{4,6},{11,9},{12,14},{19,17},{20,22},{27,25},{28,30}} | collective-permute-start | bytes 1572872 | tf_op jit(solution)/shard_map/ppermute | solution.py:281
  19.1 5.3 %collective-permute-start.3 = (f32[64,2048]{1,0:T(8,128)S(1)}, f32[64,2048]{1,0:T(8,128)S(1)}, u32[]{:S(2)}, u32[]{:S(2)}) collective-permute-start(f32[64,2048]{1,0:T(8,128)S(1)} %project.3.refs_0_), channel_id=1, source_target_pairs={{2,1},{7,6},{10,9},{15,14},{18,17},{23,22},{26,25},{31,30}} | collective-permute-start | bytes 1572872 | tf_op jit(solution)/shard_map/ppermute | solution.py:281
  19.8 13.6 %collective-permute-start.4 = (f32[64,2048]{1,0:T(8,128)S(1)}, f32[64,2048]{1,0:T(8,128)S(1)}, u32[]{:S(2)}, u32[]{:S(2)}) collective-permute-start(f32[64,2048]{1,0:T(8,128)S(1)} %project.3.refs_0_), channel_id=1, source_target_pairs={{0,1},{5,6},{8,9},{13,14},{16,17},{21,22},{24,25},{29,30}} | collective-permute-start | bytes 1572872 | tf_op jit(solution)/shard_map/ppermute | solution.py:281
  22.3 11.1 %collective-permute-start.5 = (f32[64,2048]{1,0:T(8,128)S(1)}, f32[64,2048]{1,0:T(8,128)S(1)}, u32[]{:S(2)}, u32[]{:S(2)}) collective-permute-start(f32[64,2048]{1,0:T(8,128)S(1)} %project.3.refs_0_), channel_id=1, source_target_pairs={{3,1},{4,6},{11,9},{12,14},{19,17},{20,22},{27,25},{28,30}} | collective-permute-start | bytes 1572872 | tf_op jit(solution)/shard_map/ppermute | solution.py:281
  35.8 7.3 %collective-permute-start.10 = (f32[16,2048]{1,0:T(8,128)S(1)}, f32[16,2048]{1,0:T(8,128)S(1)}, u32[]{:S(2)}, u32[]{:S(2)}) collective-permute-start(f32[16,2048]{1,0:T(8,128)S(1)} %get-tuple-element.9), channel_id=1, source_target_pairs={{1,0},{6,5},{9,8},{14,13},{17,16},{22,21},{25,24},{30,29}} | collective-permute-start | bytes 393224 | tf_op jit(solution)/shard_map/ppermute | solution.py:287
  37.1 6.7 %collective-permute-start.11 = (f32[16,2048]{1,0:T(8,128)S(1)}, f32[16,2048]{1,0:T(8,128)S(1)}, u32[]{:S(2)}, u32[]{:S(2)}) collective-permute-start(f32[16,2048]{1,0:T(8,128)S(1)} %get-tuple-element.9), channel_id=1, source_target_pairs={{1,3},{6,4},{9,11},{14,12},{17,19},{22,20},{25,27},{30,28}} | collective-permute-start | bytes 393224 | tf_op jit(solution)/shard_map/ppermute | solution.py:287
  37.8 6.0 %collective-permute-start.9 = (f32[16,2048]{1,0:T(8,128)S(1)}, f32[16,2048]{1,0:T(8,128)S(1)}, u32[]{:S(2)}, u32[]{:S(2)}) collective-permute-start(f32[16,2048]{1,0:T(8,128)S(1)} %get-tuple-element.9), channel_id=1, source_target_pairs={{1,2},{6,7},{9,10},{14,15},{17,18},{22,23},{25,26},{30,31}} | collective-permute-start | bytes 393224 | tf_op jit(solution)/shard_map/ppermute | solution.py:287
  38.5 8.4 %collective-permute-start.6 = (f32[16,2048]{1,0:T(8,128)S(1)}, f32[16,2048]{1,0:T(8,128)S(1)}, u32[]{:S(2)}, u32[]{:S(2)}) collective-permute-start(f32[16,2048]{1,0:T(8,128)S(1)} %get-tuple-element.8), channel_id=1, source_target_pairs={{1,2},{6,7},{9,10},{14,15},{17,18},{22,23},{25,26},{30,31}} | collective-permute-start | bytes 393224 | tf_op jit(solution)/shard_map/ppermute | solution.py:287
  39.2 9.2 %collective-permute-start.7 = (f32[16,2048]{1,0:T(8,128)S(1)}, f32[16,2048]{1,0:T(8,128)S(1)}, u32[]{:S(2)}, u32[]{:S(2)}) collective-permute-start(f32[16,2048]{1,0:T(8,128)S(1)} %get-tuple-element.8), channel_id=1, source_target_pairs={{1,0},{6,5},{9,8},{14,13},{17,16},{22,21},{25,24},{30,29}} | collective-permute-start | bytes 393224 | tf_op jit(solution)/shard_map/ppermute | solution.py:287
  43.2 5.2 %collective-permute-start.8 = (f32[16,2048]{1,0:T(8,128)S(1)}, f32[16,2048]{1,0:T(8,128)S(1)}, u32[]{:S(2)}, u32[]{:S(2)}) collective-permute-start(f32[16,2048]{1,0:T(8,128)S(1)} %get-tuple-element.8), channel_id=1, source_target_pairs={{1,3},{6,4},{9,11},{14,12},{17,19},{22,20},{25,27},{30,28}} | collective-permute-start | bytes 393224 | tf_op jit(solution)/shard_map/ppermute | solution.py:287
  43.9 6.3 %collective-permute-start.13 = (f32[16,2048]{1,0:T(8,128)S(1)}, f32[16,2048]{1,0:T(8,128)S(1)}, u32[]{:S(2)}, u32[]{:S(2)}) collective-permute-start(f32[16,2048]{1,0:T(8,128)S(1)} %add_select_fusion.refs_1_), channel_id=1, source_target_pairs={{0,8},{4,12},{8,0},{12,4},{16,24},{20,28},{24,16},{28,20},{1,9},{5... | collective-permute-start | bytes 393224 | tf_op jit(solution)/shard_map/ppermute | solution.py:295
  45.4 9.2 %collective-permute-start.15 = (f32[16,2048]{1,0:T(8,128)S(1)}, f32[16,2048]{1,0:T(8,128)S(1)}, u32[]{:S(2)}, u32[]{:S(2)}) collective-permute-start(f32[16,2048]{1,0:T(8,128)S(1)} %add_select_fusion.refs_1_), channel_id=1, source_target_pairs={{0,16},{4,20},{8,24},{12,28},{16,0},{20,4},{24,8},{28,12},{1,17},{... | collective-permute-start | bytes 393224 | tf_op jit(solution)/shard_map/ppermute | solution.py:295
  47.0 9.1 %collective-permute-start.17 = (f32[16,2048]{1,0:T(8,128)S(1)}, f32[16,2048]{1,0:T(8,128)S(1)}, u32[]{:S(2)}, u32[]{:S(2)}) collective-permute-start(f32[16,2048]{1,0:T(8,128)S(1)} %add_select_fusion.refs_1_), channel_id=1, source_target_pairs={{0,24},{4,28},{8,16},{12,20},{16,8},{20,12},{24,0},{28,4},{1,25},{... | collective-permute-start | bytes 393224 | tf_op jit(solution)/shard_map/ppermute | solution.py:295
  48.4 7.7 %collective-permute-start.19 = (f32[16,2048]{1,0:T(8,128)S(1)}, f32[16,2048]{1,0:T(8,128)S(1)}, u32[]{:S(2)}, u32[]{:S(2)}) collective-permute-start(f32[16,2048]{1,0:T(8,128)S(1)} %add_select_fusion.refs_1_), channel_id=1, source_target_pairs={{0,4},{4,0},{8,12},{12,8},{16,20},{20,16},{24,28},{28,24},{1,5},{5... | collective-permute-start | bytes 393224 | tf_op jit(solution)/shard_map/ppermute | solution.py:306
  48.4 8.2 %collective-permute-start.12 = (f32[16,2048]{1,0:T(8,128)S(1)}, f32[16,2048]{1,0:T(8,128)S(1)}, u32[]{:S(2)}, u32[]{:S(2)}) collective-permute-start(f32[16,2048]{1,0:T(8,128)S(1)} %add_select_fusion.1.refs_0_), channel_id=1, source_target_pairs={{0,8},{4,12},{8,0},{12,4},{16,24},{20,28},{24,16},{28,20},{1,9},{5... | collective-permute-start | bytes 393224 | tf_op jit(solution)/shard_map/ppermute | solution.py:295
  50.1 7.2 %collective-permute-start.14 = (f32[16,2048]{1,0:T(8,128)S(1)}, f32[16,2048]{1,0:T(8,128)S(1)}, u32[]{:S(2)}, u32[]{:S(2)}) collective-permute-start(f32[16,2048]{1,0:T(8,128)S(1)} %add_select_fusion.1.refs_0_), channel_id=1, source_target_pairs={{0,16},{4,20},{8,24},{12,28},{16,0},{20,4},{24,8},{28,12},{1,17},{... | collective-permute-start | bytes 393224 | tf_op jit(solution)/shard_map/ppermute | solution.py:295
  54.6 6.2 %collective-permute-start.16 = (f32[16,2048]{1,0:T(8,128)S(1)}, f32[16,2048]{1,0:T(8,128)S(1)}, u32[]{:S(2)}, u32[]{:S(2)}) collective-permute-start(f32[16,2048]{1,0:T(8,128)S(1)} %add_select_fusion.1.refs_0_), channel_id=1, source_target_pairs={{0,24},{4,28},{8,16},{12,20},{16,8},{20,12},{24,0},{28,4},{1,25},{... | collective-permute-start | bytes 393224 | tf_op jit(solution)/shard_map/ppermute | solution.py:295
  56.1 4.7 %collective-permute-start.18 = (f32[16,2048]{1,0:T(8,128)S(1)}, f32[16,2048]{1,0:T(8,128)S(1)}, u32[]{:S(2)}, u32[]{:S(2)}) collective-permute-start(f32[16,2048]{1,0:T(8,128)S(1)} %add_select_fusion.1.refs_0_), channel_id=1, source_target_pairs={{0,4},{4,0},{8,12},{12,8},{16,20},{20,16},{24,28},{28,24},{1,5},{5... | collective-permute-start | bytes 393224 | tf_op jit(solution)/shard_map/ppermute | solution.py:306
  56.1 5.2 %collective-permute-start.21 = (f32[16,2048]{1,0:T(8,128)S(1)}, f32[16,2048]{1,0:T(8,128)S(1)}, u32[]{:S(2)}, u32[]{:S(2)}) collective-permute-start(f32[16,2048]{1,0:T(8,128)S(1)} %collective-permute-done.13.refs_3_), channel_id=1, source_target_pairs={{0,4},{4,0},{8,12},{12,8},{16,20},{20,16},{24,28},{28,24},{1,5},{5... | collective-permute-start | bytes 393224 | tf_op jit(solution)/shard_map/ppermute | solution.py:306
  56.6 4.8 %collective-permute-start.23 = (f32[16,2048]{1,0:T(8,128)S(1)}, f32[16,2048]{1,0:T(8,128)S(1)}, u32[]{:S(2)}, u32[]{:S(2)}) collective-permute-start(f32[16,2048]{1,0:T(8,128)S(1)} %collective-permute-done.15.refs_5_), channel_id=1, source_target_pairs={{0,4},{4,0},{8,12},{12,8},{16,20},{20,16},{24,28},{28,24},{1,5},{5... | collective-permute-start | bytes 393224 | tf_op jit(solution)/shard_map/ppermute | solution.py:306
  57.3 4.1 %collective-permute-start.25 = (f32[16,2048]{1,0:T(8,128)S(1)}, f32[16,2048]{1,0:T(8,128)S(1)}, u32[]{:S(2)}, u32[]{:S(2)}) collective-permute-start(f32[16,2048]{1,0:T(8,128)S(1)} %collective-permute-done.17.refs_7_), channel_id=1, source_target_pairs={{0,4},{4,0},{8,12},{12,8},{16,20},{20,16},{24,28},{28,24},{1,5},{5... | collective-permute-start | bytes 393224 | tf_op jit(solution)/shard_map/ppermute | solution.py:306
  60.8 1.5 %collective-permute-start.22 = (f32[16,2048]{1,0:T(8,128)S(1)}, f32[16,2048]{1,0:T(8,128)S(1)}, u32[]{:S(2)}, u32[]{:S(2)}) collective-permute-start(f32[16,2048]{1,0:T(8,128)S(1)} %collective-permute-done.14.refs_4_), channel_id=1, source_target_pairs={{0,4},{4,0},{8,12},{12,8},{16,20},{20,16},{24,28},{28,24},{1,5},{5... | collective-permute-start | bytes 393224 | tf_op jit(solution)/shard_map/ppermute | solution.py:306
  (3 other events, 21.0 us)

commit v2 on v1

--- a/solution.py
+++ b/solution.py
@@ -23,59 +23,49 @@
     return pltpu.with_memory_space_constraint(x, pltpu.VMEM)
 
 
-def project_kernel(rows, x_ref, w_ref, out_ref, x_buf, w_buf, x_sem, w_sem):
-    n = x_buf.shape[0]
+def project_kernel(blocks, cuts, x_ref, w_ref, *refs):
+    out_refs = refs[: len(cuts)]
+    x_buf, w_buf, x_sem, w_sem = refs[len(cuts) :]
+    n = len(blocks)
     weights = pltpu.make_async_copy(w_ref, w_buf, w_sem)
     weights.start()
-    halves = 2 if rows % 2 == 0 else 1
-    size = rows // halves
     copies = [
-        [
-            pltpu.make_async_copy(
-                x_ref.at[pl.ds(i * rows + h * size, size)],
-                x_buf.at[i, pl.ds(h * size, size)],
-                x_sem.at[i, h],
-            )
-            for h in range(halves)
-        ]
-        for i in range(n)
+        pltpu.make_async_copy(
+            x_ref.at[pl.ds(first, rows)], x_buf.at[pl.ds(first, rows)], x_sem.at[i]
+        )
+        for i, (first, rows) in enumerate(blocks)
     ]
 
-    def start(i):
-        if i < n:
-            for copy in copies[i]:
-                copy.start()
-
-    start(0)
+    for copy in copies[:2]:
+        copy.start()
     weights.wait()
-    copies[0][0].wait()
-    start(1)
-    for copy in copies[0][1:]:
-        copy.wait()
-    for i in range(n):
-        if i > 0:
-            for copy in copies[i]:
-                copy.wait()
-        start(i + 2 if i > 0 else 2)
-        out_ref[:, i * rows : (i + 1) * rows] = lax.dot_general(
-            w_buf[...], x_buf[i], NT, preferred_element_type=jnp.float32
-        )
-
-
-def project(x, w, rows):
+    for i, (first, rows) in enumerate(blocks):
+        copies[i].wait()
+        if i + 2 < n:
+            copies[i + 2].start()
+        product = lax.dot_general(
+            w_buf[...], x_buf[pl.ds(first, rows)], NT, preferred_element_type=jnp.float32
+        )
+        begin = 0
+        for cut, out_ref in zip(cuts, out_refs):
+            if begin <= first < begin + cut:
+                out_ref[:, first - begin : first - begin + rows] = product
+            begin += cut
+
+
+def project(x, w, blocks, cuts):
     tokens, depth = x.shape
     width = w.shape[0]
-    rows = rows if tokens % rows == 0 else tokens
-    n = tokens // rows
+    firsts = [sum(blocks[:i]) for i in range(len(blocks))]
     return pl.pallas_call(
-        functools.partial(project_kernel, rows),
+        functools.partial(project_kernel, list(zip(firsts, blocks)), cuts),
         in_specs=[HBM, HBM],
-        out_specs=VMEM,
-        out_shape=pltpu.VMEM((width, tokens), jnp.float32),
+        out_specs=[VMEM] * len(cuts),
+        out_shape=[pltpu.VMEM((width, cut), jnp.float32) for cut in cuts],
         scratch_shapes=[
-            pltpu.VMEM((n, rows, depth), x.dtype),
+            pltpu.VMEM((tokens, depth), x.dtype),
             pltpu.VMEM((width, depth), w.dtype),
-            pltpu.SemaphoreType.DMA((n, 2)),
+            pltpu.SemaphoreType.DMA((len(blocks),)),
             pltpu.SemaphoreType.DMA,
         ],
         cost_estimate=pl.CostEstimate(
@@ -140,9 +130,11 @@
     )(segment_ids, *parts)
 
 
-def outer_kernel(n, examples, left_ref, scale_ref, *refs):
+def outer_kernel(n, examples, first, last, left_ref, scale_ref, *refs):
+    if first > 0:
+        before_ref, *refs = refs
     input_refs, out_refs = refs[:n], refs[n:]
-    width = input_refs[0].shape[0]
+    width, tokens = input_refs[0].shape
     right = jnp.concatenate(split(total(input_refs)), axis=0)
     scale = scale_ref[:, :width]
     half = width * examples
@@ -150,29 +142,39 @@
     rows = rank * examples
     for k, out_ref in enumerate(out_refs):
 
-        def dot(first):
+        def dot(row):
             return lax.dot_general(
-                left_ref[first : first + rows, :], right, NT, preferred_element_type=jnp.float32
+                left_ref[row : row + rows, first : first + tokens],
+                right,
+                NT,
+                preferred_element_type=jnp.float32,
             )
 
         high, low = dot(k * rows), dot(half + k * rows)
-        sums = high[:, :width] + high[:, width:] + low[:, :width]
+        sums = high[:, :width] + high[:, width:] + low[:, :width] + low[:, width:]
+        if first > 0:
+            sums = sums + before_ref[k * rows : (k + 1) * rows, :]
+        if not last:
+            out_ref[...] = sums
+            continue
         for i in range(rank):
             out_ref[:, i * width : (i + 1) * width] = (
                 sums[i * examples : (i + 1) * examples] * scale
             )
 
 
-def outer_sums(left, scale, inputs, cuts):
+def outer_sums(left, scale, inputs, first, before, cuts):
     examples = scale.shape[0]
-    rows, tokens = left.shape
-    width = inputs[0].shape[0]
+    rows = left.shape[0]
+    width, tokens = inputs[0].shape
     n = len(inputs)
+    shapes = [(examples, width * width // cuts)] * cuts if cuts else [(width * examples, width)]
+    operands = [left, scale] + ([before] if first > 0 else [])
     return pl.pallas_call(
-        functools.partial(outer_kernel, n, examples),
-        in_specs=[VMEM] * (2 + n),
-        out_specs=[VMEM] * cuts,
-        out_shape=[pltpu.VMEM((examples, width * width // cuts), jnp.float32)] * cuts,
+        functools.partial(outer_kernel, n, examples, first, bool(cuts)),
+        in_specs=[VMEM] * (len(operands) + n),
+        out_specs=[VMEM] * len(shapes),
+        out_shape=[pltpu.VMEM(shape, jnp.float32) for shape in shapes],
         cost_estimate=pl.CostEstimate(
             flops=4 * rows * tokens * width,
             bytes_accessed=2 * rows * tokens,
@@ -180,23 +182,28 @@
         ),
         compiler_params=pltpu.CompilerParams(vmem_limit_bytes=24 << 20),
         name="outer_sums",
-    )(in_vmem(left), in_vmem(scale), *inputs)
+    )(*[in_vmem(x) for x in operands], *inputs)
 
 
 def gram_kernel(n, cuts, row_count, examples, block, first_ref, *refs):
     parts = refs[: n * cuts]
-    features_ref, out_ref, terms, rows_ref, out_sem = refs[n * cuts :]
+    features_ref, out_ref, terms, rows_ref, out_sem, features_sem = refs[n * cuts :]
     size = parts[0].shape[1]
     total_examples = n * examples
+    copies = [
+        pltpu.make_async_copy(
+            parts[c], features_ref.at[:, pl.ds(c * size, size)], features_sem.at[c]
+        )
+        for c in range(cuts)
+    ]
+    for copy in copies:
+        copy.start()
     for k in range(n):
         high = slice(k * examples, (k + 1) * examples)
         low = slice(total_examples + k * examples, total_examples + (k + 1) * examples)
         for c in range(cuts):
             columns = slice(c * size, (c + 1) * size)
-            part = parts[k * cuts + c][...]
-            if k == 0:
-                features_ref[:, columns] = part
-            terms[high, columns], terms[low, columns] = split(part)
+            terms[high, columns], terms[low, columns] = split(parts[k * cuts + c][...])
     lanes = rows_ref.shape[0]
     first = first_ref[0]
     base = pl.multiple_of(first // lanes * lanes, lanes)
@@ -210,7 +217,6 @@
             a, b, (((1,), (0,)), ((), ())), preferred_element_type=jnp.float32
         )
 
-    copies = []
     for k in range(out_ref.shape[1] // block):
         columns = slice(k * block, (k + 1) * block)
         product = dot(left_twice, terms[:, columns]) + dot(
@@ -235,7 +241,7 @@
     return pl.pallas_call(
         functools.partial(gram_kernel, n, cuts, row_count, examples, block),
         in_specs=[SMEM] + [VMEM] * (n * cuts),
-        out_specs=[VMEM, HBM],
+        out_specs=[HBM, HBM],
         out_shape=[
             jax.ShapeDtypeStruct((examples, size), jnp.float32),
             jax.ShapeDtypeStruct((row_count, size), jnp.float32),
@@ -244,6 +250,7 @@
             pltpu.VMEM((2 * n * examples, size), jnp.bfloat16),
             pltpu.VMEM((max(row_count, 128), size), jnp.float32),
             pltpu.SemaphoreType.DMA((size // block,)),
+            pltpu.SemaphoreType.DMA((cuts,)),
         ],
         cost_estimate=pl.CostEstimate(
             flops=6 * n * examples * row_count * size,
@@ -308,15 +315,19 @@
     d, m = lax.axis_index("dp"), lax.axis_index("mp")
     is_owner = m == jnp.minimum((model - 1) // 2 + d % pair, model - 1)
 
-    outputs = project(out_grad, proj_out, 1024)
+    tokens = hidden.shape[0]
+    unit = tokens // 8
+    (outputs,) = project(out_grad, proj_out, [4 * unit, 4 * unit], (tokens,))
     outputs_sent = to_owner(outputs)
-    inputs = project(hidden, proj_in, 512)
-    inputs_sent = to_owner(inputs)
+    inputs = project(hidden, proj_in, [2 * unit] * 4, (6 * unit, 2 * unit))
+    early = to_owner(inputs[0])
+    late = to_owner(inputs[1])
     left, scale = expand(segment_ids, outputs_sent, EX_DEV)
+    (sums,) = outer_sums(left, scale, early, 0, None, 0)
     pieces = []
-    for summed in outer_sums(left, scale, inputs_sent, 2):
+    for summed in outer_sums(left, scale, late, 6 * unit, sums, 2):
         features = jnp.where(is_owner, summed, sum(from_owner(summed)))
-        parts = [features] + [across(features, k) for k in range(1, groups)]
+        parts = [features] + [across(features, k) for k in sorted(range(1, groups), key=lambda k: -bin(k).count("1"))]
         if pair == 2:
             parts = parts + [swap(x) for x in parts]
         pieces.append(parts)

time: 65.8 us -> 70.8 us (1.076)
  starting transfers between devices: 25.4 us -> 33.7 us
  waiting for transfers between devices: 21.1 us -> 19.2 us
  Pallas kernels: 18 us -> 16.6 us
    ppermute x6 -> x9, starting transfers between devices: 10.8 us -> 18.5 us  [to_owner(): lax.ppermute(x, axes, [(at(d, m), at(d, 0)) for d in range(data)])]
    ppermute x6, waiting for transfers between devices: 7.24 us -> 6.27 us  [across(): lax.ppermute(x, 'dp', [(g * pair + c, other(g, k) * pair + c) for g in ra...]
    ppermute x6 -> x9, waiting for transfers between devices: 8.93 us -> 8.03 us  [to_owner(): lax.ppermute(x, axes, [(at(d, m), at(d, 0)) for d in range(data)])]
    pallas_call x3 -> x4, Pallas kernels: 13.9 us -> 13.2 us  [the longest x2 10.5 us: project(): pl.pallas_call(functools.partial(project_kernel, list(zip(firsts, blocks)...]
  transfers between devices with their start and end apart: 26 -> 29, of which waited for: 10 -> 10; matrix products, arithmetic and copies ran while one was open for 0% -> 0% of each run, Pallas kernels for 13% -> 10%
where the time goes in v2:
time: 70.8 us; the launch traced here: 70.4 us
  starting transfers between devices  33.7 us (48%)
  waiting for transfers between devices  19.2 us (27%)
  Pallas kernels  16.6 us (23%)
  between operations  0.89 us (1%)
    ppermute x9, starting transfers between devices, to_owner(): lax.ppermute(x, axes, [(at(d, m), at(d, 0)) for d in range(data)])  18.5 us
    pallas_call x2, Pallas kernels, project(): pl.pallas_call(functools.partial(project_kernel, list(zip(firsts, blocks)...  10.5 us
    ppermute x6, starting transfers between devices, across(): lax.ppermute(x, 'dp', [(g * pair + c, other(g, k) * pair + c) for g in ra...  8.12 us
    ppermute x9, waiting for transfers between devices, to_owner(): lax.ppermute(x, axes, [(at(d, m), at(d, 0)) for d in range(data)])  8.03 us
    ppermute x6, waiting for transfers between devices, across(): lax.ppermute(x, 'dp', [(g * pair + c, other(g, k) * pair + c) for g in ra...  6.27 us
    ppermute x6, starting transfers between devices, from_owner(): lax.ppermute(x, axes, [(at(d, 0), at(d, m)) for d in range(data)])  5.25 us
    ppermute x6, waiting for transfers between devices, from_owner(): lax.ppermute(x, axes, [(at(d, 0), at(d, m)) for d in range(data)])  3.63 us
    pallas_call x2, Pallas kernels, outer_sums(): pl.pallas_call(functools.partial(outer_kernel, n, examples, first, bool(c...  2.74 us
  transfers between devices with their start and end apart: 29, of which 10 were waited for; matrix products, arithmetic and copies ran while one was open for 0% of the time, Pallas kernels for 10%

profile of v2, /device:TPU:0, one launch (start us, length us, event | category | flops | bytes accessed | tf_op | source)
XLA Modules:
  0.0 70.4 jit_solution(12206608333712619893)
XLA Ops:
  0.6 6.9 %project.3 = (f32[64,1536]{1,0:T(8,128)S(1)}, f32[64,512]{1,0:T(8,128)S(1)}) custom-call(bf16[2048,3456]{1,0:T(8,128)(2,1)} %x_ref.3, bf16[64,3456]{1,0:T(8,128)(2,1)} %w_ref.3), custom_call_target="tpu_custom_call" | custom-call | flops 905969664 | bytes 14155776 | tf_op jit(solution)/shard_map/project/pallas_call | solution.py:60
  8.2 3.6 %project.2.refs_0_ = f32[64,2048]{1,0:T(8,128)S(1)} custom-call(bf16[2048,1280]{1,0:T(8,128)(2,1)} %x_ref.2, bf16[64,1280]{1,0:T(8,128)(2,1)} %w_ref.2), custom_call_target="tpu_custom_call" | custom-call | flops 335544320 | bytes 5242880 | tf_op jit(solution)/shard_map/project/pallas_call | solution.py:60
  11.8 0.7 collective-permute-start
  12.5 6.2 %collective-permute-start.1 = (f32[64,2048]{1,0:T(8,128)S(1)}, f32[64,2048]{1,0:T(8,128)S(1)}, u32[]{:S(2)}, u32[]{:S(2)}) collective-permute-start(f32[64,2048]{1,0:T(8,128)S(1)} %project.2.refs_0_), channel_id=1, source_target_pairs={{0,1},{5,6},{8,9},{13,14},{16,17},{21,22},{24,25},{29,30}} | collective-permute-start | bytes 1572872 | tf_op jit(solution)/shard_map/ppermute | solution.py:288
  18.7 0.7 collective-permute-start.2
  19.4 1.9 %collective-permute-start.4 = (f32[64,1536]{1,0:T(8,128)S(1)}, f32[64,1536]{1,0:T(8,128)S(1)}, u32[]{:S(2)}, u32[]{:S(2)}) collective-permute-start(f32[64,1536]{1,0:T(8,128)S(1)} %get-tuple-element.10.refs_0_), channel_id=1, source_target_pairs={{0,1},{5,6},{8,9},{13,14},{16,17},{21,22},{24,25},{29,30}} | collective-permute-start | bytes 1179656 | tf_op jit(solution)/shard_map/ppermute | solution.py:288
  22.7 7.1 %collective-permute-done.1.refs_2_ = f32[64,2048]{1,0:T(8,128)S(1)} collective-permute-done((f32[64,2048]{1,0:T(8,128)S(1)}, f32[64,2048]{1,0:T(8,128)S(1)}, u32[]{:S(2)}, u32[]{:S(2)}) %collective-permute-start.1) | collective-permute-done | bytes 524320 | tf_op jit(solution)/shard_map/ppermute | solution.py:288
  29.8 6.3 %collective-permute-start.7 = (f32[64,512]{1,0:T(8,128)S(1)}, f32[64,512]{1,0:T(8,128)S(1)}, u32[]{:S(2)}, u32[]{:S(2)}) collective-permute-start(f32[64,512]{1,0:T(8,128)S(1)} %get-tuple-element.11.refs_1_), channel_id=1, source_target_pairs={{0,1},{5,6},{8,9},{13,14},{16,17},{21,22},{24,25},{29,30}} | collective-permute-start | bytes 393224 | tf_op jit(solution)/shard_map/ppermute | solution.py:288
  36.8 1.4 %expand.1 = (bf16[2048,2048]{1,0:T(8,128)(2,1)S(1)}, f32[16,128]{1,0:T(8,128)S(1)}) custom-call(s32[1,2048]{1,0:T(1,128)S(1)} %copy-done, f32[64,2048]{1,0:T(8,128)S(1)} %project.2.refs_0_, f32[64,2048]{1,0:T(8,128)S(1)} %collective-permute-done.refs_1_, f32[64,2048]{1,0:T(8,128)S(1)} %collective-permute-done.1.refs_2_, ...), custom_call_target="tpu_custom_call" | custom-call | flops 8388608 | bytes 8388608 | tf_op jit(solution)/shard_map/expand/pallas_call | solution.py:115
  38.3 1.9 %outer_sums.2.refs_0_ = f32[1024,64]{1,0:T(8,128)S(1)} custom-call(bf16[2048,2048]{1,0:T(8,128)(2,1)S(1)} %get-tuple-element.8.left_ref, f32[16,128]{1,0:T(8,128)S(1)} %get-tuple-element.9.scale_ref, f32[64,1536]{1,0:T(8,128)S(1)} %get-tuple-element.10.refs_0_, f32[64,1536]{1,0:T(8,128)S(1)} %collective-permute-done.3.refs_1_, ...), custom_call_target="tpu_custom_call" | custom-call | flops 805306368 | bytes 6291456 | tf_op jit(solution)/shard_map/outer_sums/pallas_call | solution.py:173
  40.1 0.9 %collective-permute-done.7.refs_3_ = f32[64,512]{1,0:T(8,128)S(1)} collective-permute-done((f32[64,512]{1,0:T(8,128)S(1)}, f32[64,512]{1,0:T(8,128)S(1)}, u32[]{:S(2)}, u32[]{:S(2)}) %collective-permute-start.7) | collective-permute-done | bytes 131104 | tf_op jit(solution)/shard_map/ppermute | solution.py:288
  41.0 0.9 %outer_sums.3 = (f32[16,2048]{1,0:T(8,128)S(1)}, f32[16,2048]{1,0:T(8,128)S(1)}) custom-call(bf16[2048,2048]{1,0:T(8,128)(2,1)S(1)} %get-tuple-element.8.left_ref, f32[16,128]{1,0:T(8,128)S(1)} %get-tuple-element.9.scale_ref, f32[1024,64]{1,0:T(8,128)S(1)} %outer_sums.2.refs_0_, f32[64,512]{1,0:T(8,128)S(1)} %get-tuple-element.11.refs_1_, ...), custom_call_target="tpu_custom_call" | custom-call | flops 268435456 | bytes 2097152 | tf_op jit(solution)/shard_map/outer_sums/pallas_call | solution.py:173
  42.6 1.3 %collective-permute-start.13 = (f32[16,2048]{1,0:T(8,128)S(1)}, f32[16,2048]{1,0:T(8,128)S(1)}, u32[]{:S(2)}, u32[]{:S(2)}) collective-permute-start(f32[16,2048]{1,0:T(8,128)S(1)} %get-tuple-element.13), channel_id=1, source_target_pairs={{1,0},{6,5},{9,8},{14,13},{17,16},{22,21},{25,24},{30,29}} | collective-permute-start | bytes 393224 | tf_op jit(solution)/shard_map/ppermute | solution.py:294
  44.6 1.3 %collective-permute-start.10 = (f32[16,2048]{1,0:T(8,128)S(1)}, f32[16,2048]{1,0:T(8,128)S(1)}, u32[]{:S(2)}, u32[]{:S(2)}) collective-permute-start(f32[16,2048]{1,0:T(8,128)S(1)} %get-tuple-element.12), channel_id=1, source_target_pairs={{1,0},{6,5},{9,8},{14,13},{17,16},{22,21},{25,24},{30,29}} | collective-permute-start | bytes 393224 | tf_op jit(solution)/shard_map/ppermute | solution.py:294
  47.2 2.7 %collective-permute-done.13 = f32[16,2048]{1,0:T(8,128)S(1)} collective-permute-done((f32[16,2048]{1,0:T(8,128)S(1)}, f32[16,2048]{1,0:T(8,128)S(1)}, u32[]{:S(2)}, u32[]{:S(2)}) %collective-permute-start.13) | collective-permute-done | bytes 131104 | tf_op jit(solution)/shard_map/ppermute | solution.py:294
  49.9 2.5 %collective-permute-start.16 = (f32[16,2048]{1,0:T(8,128)S(1)}, f32[16,2048]{1,0:T(8,128)S(1)}, u32[]{:S(2)}, u32[]{:S(2)}) collective-permute-start(f32[16,2048]{1,0:T(8,128)S(1)} %add_select_fusion.refs_1_), channel_id=1, source_target_pairs={{0,24},{4,28},{8,16},{12,20},{16,8},{20,12},{24,0},{28,4},{1,25},{... | collective-permute-start | bytes 393224 | tf_op jit(solution)/shard_map/ppermute | solution.py:302
  53.0 0.9 %collective-permute-done.10 = f32[16,2048]{1,0:T(8,128)S(1)} collective-permute-done((f32[16,2048]{1,0:T(8,128)S(1)}, f32[16,2048]{1,0:T(8,128)S(1)}, u32[]{:S(2)}, u32[]{:S(2)}) %collective-permute-start.10) | collective-permute-done | bytes 131104 | tf_op jit(solution)/shard_map/ppermute | solution.py:294
  53.9 1.5 %collective-permute-start.20 = (f32[16,2048]{1,0:T(8,128)S(1)}, f32[16,2048]{1,0:T(8,128)S(1)}, u32[]{:S(2)}, u32[]{:S(2)}) collective-permute-start(f32[16,2048]{1,0:T(8,128)S(1)} %add_select_fusion.refs_1_), channel_id=1, source_target_pairs={{0,16},{4,20},{8,24},{12,28},{16,0},{20,4},{24,8},{28,12},{1,17},{... | collective-permute-start | bytes 393224 | tf_op jit(solution)/shard_map/ppermute | solution.py:302
  55.8 2.5 %collective-permute-start.15 = (f32[16,2048]{1,0:T(8,128)S(1)}, f32[16,2048]{1,0:T(8,128)S(1)}, u32[]{:S(2)}, u32[]{:S(2)}) collective-permute-start(f32[16,2048]{1,0:T(8,128)S(1)} %add_select_fusion.1.refs_0_), channel_id=1, source_target_pairs={{0,24},{4,28},{8,16},{12,20},{16,8},{20,12},{24,0},{28,4},{1,25},{... | collective-permute-start | bytes 393224 | tf_op jit(solution)/shard_map/ppermute | solution.py:302
  59.4 4.4 %collective-permute-done.20.refs_7_ = f32[16,2048]{1,0:T(8,128)S(1)} collective-permute-done((f32[16,2048]{1,0:T(8,128)S(1)}, f32[16,2048]{1,0:T(8,128)S(1)}, u32[]{:S(2)}, u32[]{:S(2)}) %collective-permute-start.20) | collective-permute-done | bytes 131104 | tf_op jit(solution)/shard_map/ppermute | solution.py:302
  64.7 1.2 %collective-permute-done.17.refs_4_ = f32[16,2048]{1,0:T(8,128)S(1)} collective-permute-done((f32[16,2048]{1,0:T(8,128)S(1)}, f32[16,2048]{1,0:T(8,128)S(1)}, u32[]{:S(2)}, u32[]{:S(2)}) %collective-permute-start.17) | collective-permute-done | bytes 131104 | tf_op jit(solution)/shard_map/ppermute | solution.py:302
  65.9 0.7 collective-permute-done.19.refs_6_
  67.2 0.7 collective-permute-done.23.refs_10_
  68.4 2.0 %gram_rows.1 = (f32[16,4096]{1,0:T(8,128)}, f32[128,4096]{1,0:T(8,128)}) custom-call(s32[1]{0:T(128)} %bitcast.first_ref, f32[16,2048]{1,0:T(8,128)S(1)} %add_select_fusion.1.refs_0_, f32[16,2048]{1,0:T(8,128)S(1)} %add_select_fusion.refs_1_, f32[16,2048]{1,0:T(8,128)S(1)} %collective-permute-done.15.refs_2_, ...), custom_call_target="tpu_custom_call" | custom-call | flops 402653184 | bytes 4194304 | tf_op jit(solution)/shard_map/gram_rows/pallas_call | solution.py:241
  (44 shorter events, 9.5 us)
Async XLA Ops:
  7.5 13.8 %collective-permute-start.3 = (f32[64,1536]{1,0:T(8,128)S(1)}, f32[64,1536]{1,0:T(8,128)S(1)}, u32[]{:S(2)}, u32[]{:S(2)}) collective-permute-start(f32[64,1536]{1,0:T(8,128)S(1)} %get-tuple-element.10.refs_0_), channel_id=1, source_target_pairs={{2,1},{7,6},{10,9},{15,14},{18,17},{23,22},{26,25},{31,30}} | collective-permute-start | bytes 1179656 | tf_op jit(solution)/shard_map/ppermute | solution.py:288
  11.8 10.2 %collective-permute-start = (f32[64,2048]{1,0:T(8,128)S(1)}, f32[64,2048]{1,0:T(8,128)S(1)}, u32[]{:S(2)}, u32[]{:S(2)}) collective-permute-start(f32[64,2048]{1,0:T(8,128)S(1)} %project.2.refs_0_), channel_id=1, source_target_pairs={{2,1},{7,6},{10,9},{15,14},{18,17},{23,22},{26,25},{31,30}} | collective-permute-start | bytes 1572872 | tf_op jit(solution)/shard_map/ppermute | solution.py:288
  12.5 17.3 %collective-permute-start.1 = (f32[64,2048]{1,0:T(8,128)S(1)}, f32[64,2048]{1,0:T(8,128)S(1)}, u32[]{:S(2)}, u32[]{:S(2)}) collective-permute-start(f32[64,2048]{1,0:T(8,128)S(1)} %project.2.refs_0_), channel_id=1, source_target_pairs={{0,1},{5,6},{8,9},{13,14},{16,17},{21,22},{24,25},{29,30}} | collective-permute-start | bytes 1572872 | tf_op jit(solution)/shard_map/ppermute | solution.py:288
  18.7 17.4 %collective-permute-start.2 = (f32[64,2048]{1,0:T(8,128)S(1)}, f32[64,2048]{1,0:T(8,128)S(1)}, u32[]{:S(2)}, u32[]{:S(2)}) collective-permute-start(f32[64,2048]{1,0:T(8,128)S(1)} %project.2.refs_0_), channel_id=1, source_target_pairs={{3,1},{4,6},{11,9},{12,14},{19,17},{20,22},{27,25},{28,30}} | collective-permute-start | bytes 1572872 | tf_op jit(solution)/shard_map/ppermute | solution.py:288
  19.4 18.8 %collective-permute-start.4 = (f32[64,1536]{1,0:T(8,128)S(1)}, f32[64,1536]{1,0:T(8,128)S(1)}, u32[]{:S(2)}, u32[]{:S(2)}) collective-permute-start(f32[64,1536]{1,0:T(8,128)S(1)} %get-tuple-element.10.refs_0_), channel_id=1, source_target_pairs={{0,1},{5,6},{8,9},{13,14},{16,17},{21,22},{24,25},{29,30}} | collective-permute-start | bytes 1179656 | tf_op jit(solution)/shard_map/ppermute | solution.py:288
  21.3 16.9 %collective-permute-start.5 = (f32[64,1536]{1,0:T(8,128)S(1)}, f32[64,1536]{1,0:T(8,128)S(1)}, u32[]{:S(2)}, u32[]{:S(2)}) collective-permute-start(f32[64,1536]{1,0:T(8,128)S(1)} %get-tuple-element.10.refs_0_), channel_id=1, source_target_pairs={{3,1},{4,6},{11,9},{12,14},{19,17},{20,22},{27,25},{28,30}} | collective-permute-start | bytes 1179656 | tf_op jit(solution)/shard_map/ppermute | solution.py:288
  22.0 18.1 %collective-permute-start.6 = (f32[64,512]{1,0:T(8,128)S(1)}, f32[64,512]{1,0:T(8,128)S(1)}, u32[]{:S(2)}, u32[]{:S(2)}) collective-permute-start(f32[64,512]{1,0:T(8,128)S(1)} %get-tuple-element.11.refs_1_), channel_id=1, source_target_pairs={{2,1},{7,6},{10,9},{15,14},{18,17},{23,22},{26,25},{31,30}} | collective-permute-start | bytes 393224 | tf_op jit(solution)/shard_map/ppermute | solution.py:288
  29.8 11.2 %collective-permute-start.7 = (f32[64,512]{1,0:T(8,128)S(1)}, f32[64,512]{1,0:T(8,128)S(1)}, u32[]{:S(2)}, u32[]{:S(2)}) collective-permute-start(f32[64,512]{1,0:T(8,128)S(1)} %get-tuple-element.11.refs_1_), channel_id=1, source_target_pairs={{0,1},{5,6},{8,9},{13,14},{16,17},{21,22},{24,25},{29,30}} | collective-permute-start | bytes 393224 | tf_op jit(solution)/shard_map/ppermute | solution.py:288
  36.1 4.9 %collective-permute-start.8 = (f32[64,512]{1,0:T(8,128)S(1)}, f32[64,512]{1,0:T(8,128)S(1)}, u32[]{:S(2)}, u32[]{:S(2)}) collective-permute-start(f32[64,512]{1,0:T(8,128)S(1)} %get-tuple-element.11.refs_1_), channel_id=1, source_target_pairs={{3,1},{4,6},{11,9},{12,14},{19,17},{20,22},{27,25},{28,30}} | collective-permute-start | bytes 393224 | tf_op jit(solution)/shard_map/ppermute | solution.py:288
  41.9 4.6 %collective-permute-start.12 = (f32[16,2048]{1,0:T(8,128)S(1)}, f32[16,2048]{1,0:T(8,128)S(1)}, u32[]{:S(2)}, u32[]{:S(2)}) collective-permute-start(f32[16,2048]{1,0:T(8,128)S(1)} %get-tuple-element.13), channel_id=1, source_target_pairs={{1,2},{6,7},{9,10},{14,15},{17,18},{22,23},{25,26},{30,31}} | collective-permute-start | bytes 393224 | tf_op jit(solution)/shard_map/ppermute | solution.py:294
  42.6 7.3 %collective-permute-start.13 = (f32[16,2048]{1,0:T(8,128)S(1)}, f32[16,2048]{1,0:T(8,128)S(1)}, u32[]{:S(2)}, u32[]{:S(2)}) collective-permute-start(f32[16,2048]{1,0:T(8,128)S(1)} %get-tuple-element.13), channel_id=1, source_target_pairs={{1,0},{6,5},{9,8},{14,13},{17,16},{22,21},{25,24},{30,29}} | collective-permute-start | bytes 393224 | tf_op jit(solution)/shard_map/ppermute | solution.py:294
  43.9 6.0 %collective-permute-start.14 = (f32[16,2048]{1,0:T(8,128)S(1)}, f32[16,2048]{1,0:T(8,128)S(1)}, u32[]{:S(2)}, u32[]{:S(2)}) collective-permute-start(f32[16,2048]{1,0:T(8,128)S(1)} %get-tuple-element.13), channel_id=1, source_target_pairs={{1,3},{6,4},{9,11},{14,12},{17,19},{22,20},{25,27},{30,28}} | collective-permute-start | bytes 393224 | tf_op jit(solution)/shard_map/ppermute | solution.py:294
  44.6 9.4 %collective-permute-start.10 = (f32[16,2048]{1,0:T(8,128)S(1)}, f32[16,2048]{1,0:T(8,128)S(1)}, u32[]{:S(2)}, u32[]{:S(2)}) collective-permute-start(f32[16,2048]{1,0:T(8,128)S(1)} %get-tuple-element.12), channel_id=1, source_target_pairs={{1,0},{6,5},{9,8},{14,13},{17,16},{22,21},{25,24},{30,29}} | collective-permute-start | bytes 393224 | tf_op jit(solution)/shard_map/ppermute | solution.py:294
  45.9 9.6 %collective-permute-start.11 = (f32[16,2048]{1,0:T(8,128)S(1)}, f32[16,2048]{1,0:T(8,128)S(1)}, u32[]{:S(2)}, u32[]{:S(2)}) collective-permute-start(f32[16,2048]{1,0:T(8,128)S(1)} %get-tuple-element.12), channel_id=1, source_target_pairs={{1,3},{6,4},{9,11},{14,12},{17,19},{22,20},{25,27},{30,28}} | collective-permute-start | bytes 393224 | tf_op jit(solution)/shard_map/ppermute | solution.py:294
  46.6 9.2 %collective-permute-start.9 = (f32[16,2048]{1,0:T(8,128)S(1)}, f32[16,2048]{1,0:T(8,128)S(1)}, u32[]{:S(2)}, u32[]{:S(2)}) collective-permute-start(f32[16,2048]{1,0:T(8,128)S(1)} %get-tuple-element.12), channel_id=1, source_target_pairs={{1,2},{6,7},{9,10},{14,15},{17,18},{22,23},{25,26},{30,31}} | collective-permute-start | bytes 393224 | tf_op jit(solution)/shard_map/ppermute | solution.py:294
  49.9 8.4 %collective-permute-start.16 = (f32[16,2048]{1,0:T(8,128)S(1)}, f32[16,2048]{1,0:T(8,128)S(1)}, u32[]{:S(2)}, u32[]{:S(2)}) collective-permute-start(f32[16,2048]{1,0:T(8,128)S(1)} %add_select_fusion.refs_1_), channel_id=1, source_target_pairs={{0,24},{4,28},{8,16},{12,20},{16,8},{20,12},{24,0},{28,4},{1,25},{... | collective-permute-start | bytes 393224 | tf_op jit(solution)/shard_map/ppermute | solution.py:302
  52.4 6.4 %collective-permute-start.18 = (f32[16,2048]{1,0:T(8,128)S(1)}, f32[16,2048]{1,0:T(8,128)S(1)}, u32[]{:S(2)}, u32[]{:S(2)}) collective-permute-start(f32[16,2048]{1,0:T(8,128)S(1)} %add_select_fusion.refs_1_), channel_id=1, source_target_pairs={{0,8},{4,12},{8,0},{12,4},{16,24},{20,28},{24,16},{28,20},{1,9},{5... | collective-permute-start | bytes 393224 | tf_op jit(solution)/shard_map/ppermute | solution.py:302
  53.9 9.8 %collective-permute-start.20 = (f32[16,2048]{1,0:T(8,128)S(1)}, f32[16,2048]{1,0:T(8,128)S(1)}, u32[]{:S(2)}, u32[]{:S(2)}) collective-permute-start(f32[16,2048]{1,0:T(8,128)S(1)} %add_select_fusion.refs_1_), channel_id=1, source_target_pairs={{0,16},{4,20},{8,24},{12,28},{16,0},{20,4},{24,8},{28,12},{1,17},{... | collective-permute-start | bytes 393224 | tf_op jit(solution)/shard_map/ppermute | solution.py:302
  55.5 8.7 %collective-permute-start.22 = (f32[16,2048]{1,0:T(8,128)S(1)}, f32[16,2048]{1,0:T(8,128)S(1)}, u32[]{:S(2)}, u32[]{:S(2)}) collective-permute-start(f32[16,2048]{1,0:T(8,128)S(1)} %add_select_fusion.refs_1_), channel_id=1, source_target_pairs={{0,4},{4,0},{8,12},{12,8},{16,20},{20,16},{24,28},{28,24},{1,5},{5... | collective-permute-start | bytes 393224 | tf_op jit(solution)/shard_map/ppermute | solution.py:313
  55.8 8.5 %collective-permute-start.15 = (f32[16,2048]{1,0:T(8,128)S(1)}, f32[16,2048]{1,0:T(8,128)S(1)}, u32[]{:S(2)}, u32[]{:S(2)}) collective-permute-start(f32[16,2048]{1,0:T(8,128)S(1)} %add_select_fusion.1.refs_0_), channel_id=1, source_target_pairs={{0,24},{4,28},{8,16},{12,20},{16,8},{20,12},{24,0},{28,4},{1,25},{... | collective-permute-start | bytes 393224 | tf_op jit(solution)/shard_map/ppermute | solution.py:302
  58.3 7.6 %collective-permute-start.17 = (f32[16,2048]{1,0:T(8,128)S(1)}, f32[16,2048]{1,0:T(8,128)S(1)}, u32[]{:S(2)}, u32[]{:S(2)}) collective-permute-start(f32[16,2048]{1,0:T(8,128)S(1)} %add_select_fusion.1.refs_0_), channel_id=1, source_target_pairs={{0,8},{4,12},{8,0},{12,4},{16,24},{20,28},{24,16},{28,20},{1,9},{5... | collective-permute-start | bytes 393224 | tf_op jit(solution)/shard_map/ppermute | solution.py:302
  58.8 7.7 %collective-permute-start.19 = (f32[16,2048]{1,0:T(8,128)S(1)}, f32[16,2048]{1,0:T(8,128)S(1)}, u32[]{:S(2)}, u32[]{:S(2)}) collective-permute-start(f32[16,2048]{1,0:T(8,128)S(1)} %add_select_fusion.1.refs_0_), channel_id=1, source_target_pairs={{0,16},{4,20},{8,24},{12,28},{16,0},{20,4},{24,8},{28,12},{1,17},{... | collective-permute-start | bytes 393224 | tf_op jit(solution)/shard_map/ppermute | solution.py:302
  63.8 2.9 %collective-permute-start.21 = (f32[16,2048]{1,0:T(8,128)S(1)}, f32[16,2048]{1,0:T(8,128)S(1)}, u32[]{:S(2)}, u32[]{:S(2)}) collective-permute-start(f32[16,2048]{1,0:T(8,128)S(1)} %add_select_fusion.1.refs_0_), channel_id=1, source_target_pairs={{0,4},{4,0},{8,12},{12,8},{16,20},{20,16},{24,28},{28,24},{1,5},{5... | collective-permute-start | bytes 393224 | tf_op jit(solution)/shard_map/ppermute | solution.py:313
  64.3 2.9 %collective-permute-start.26 = (f32[16,2048]{1,0:T(8,128)S(1)}, f32[16,2048]{1,0:T(8,128)S(1)}, u32[]{:S(2)}, u32[]{:S(2)}) collective-permute-start(f32[16,2048]{1,0:T(8,128)S(1)} %collective-permute-done.18.refs_5_), channel_id=1, source_target_pairs={{0,4},{4,0},{8,12},{12,8},{16,20},{20,16},{24,28},{28,24},{1,5},{5... | collective-permute-start | bytes 393224 | tf_op jit(solution)/shard_map/ppermute | solution.py:313
  (6 other events, 44.5 us)
